TPU v7x, 32 devices: a whole 2x2x4 slice. The times are simulated.
32 devices in a mesh: grp: 2 (over x), layer: 4 (over z), feat: 4 (over y, core).
Axes of the slice: x: 2, y: 2, z: 4, core: 2. Of those that a mesh axis runs over, the one named last changes fastest.
Arguments:
- inputs: bfloat16 [4, 512, 2304], P('layer', ('grp', 'feat')), may hold values from -6 to 6
- targets: bfloat16 [512, 4, 2304], P(('grp', 'feat'), None, 'layer'), may hold values from -6 to 6
- enc_weight: bfloat16 [4, 2304, 8192], P('layer', None, 'feat'), may hold values from -0.125 to 0.125
- enc_bias: float32 [4, 8192], P('layer', 'feat'), may hold values from -3 to 3
- dec_weight: bfloat16 [10, 8192, 2304], P(None, 'feat', 'layer'), may hold values from -0.0625 to 0.0625
- dec_bias: float32 [4, 2304], P(None, 'layer'), may hold values from -3 to 3
Outputs:
- enc_grad: bfloat16 [4, 2304, 8192], P('layer', 'grp', 'feat')
- enc_bias_grad: float32 [4, 8192], P('layer', 'feat')
- dec_grad: bfloat16 [10, 8192, 2304], P('grp', 'feat', 'layer')
- dec_bias_grad: float32 [4, 2304], P(None, 'layer')
All inputs are finite; a program needn't handle non-finite values.
Results may differ from a plain program's by a relative error of at most 0.019.
Values may be sent and summed in bfloat16 or wider, within the bound.
A program may use at most 128 MiB of HBM per device.

v0:
```python
import jax
import jax.numpy as jnp
from jax import lax
from jax.sharding import PartitionSpec as P


def pair_list(count):
    return [(source, target) for source in range(count) for target in range(source, count)]


def per_device(inputs, targets, enc_weight, enc_bias, dec_weight, dec_bias):
    layers = lax.axis_size("layer")
    feat_count = lax.axis_size("feat")
    group_count = lax.axis_size("grp")
    pairs = pair_list(layers)
    tok_dev = inputs.shape[1]
    total_tokens = tok_dev * feat_count * group_count
    rows = lax.all_gather(inputs[0], "feat", axis=0, tiled=True)
    pre = jnp.dot(rows, enc_weight[0], preferred_element_type=jnp.float32) + enc_bias[0]
    acts = jnp.maximum(pre, 0.0).astype(jnp.bfloat16)
    sources = lax.all_gather(acts[None], "layer", axis=0, tiled=True)

    def decode_target(block, target):
        total = jnp.zeros((block.shape[1], dec_weight.shape[2]), jnp.float32)
        for index, (source, later) in enumerate(pairs):
            if later == target:
                total = total + jnp.dot(
                    block[source], dec_weight[index], preferred_element_type=jnp.float32
                )
        return total

    def partial_rows():
        return jnp.stack([decode_target(sources, target) for target in range(layers)], axis=1)

    recon = lax.psum_scatter(
        partial_rows().astype(jnp.bfloat16), "feat", scatter_dimension=0, tiled=True
    ).astype(jnp.float32)
    errors = recon + dec_bias - targets.astype(jnp.float32)
    dec_bias_grad = lax.psum(jnp.sum(errors, axis=0), ("grp", "feat")) / total_tokens
    derr = lax.all_gather((errors / total_tokens).astype(jnp.bfloat16), "feat", axis=0, tiled=True)
    all_sources = lax.all_gather(sources, "grp", axis=1, tiled=True)
    all_errors = lax.all_gather(derr, "grp", axis=0, tiled=True)
    per_group = len(pairs) // group_count

    def make_branch(group):

        def branch_fn():
            chosen = pairs[group * per_group : (group + 1) * per_group]
            return jnp.stack(
                [
                    jnp.einsum(
                        "rf,rd->fd",
                        all_sources[s],
                        all_errors[:, t, :],
                        preferred_element_type=jnp.float32,
                    )
                    for s, t in chosen
                ]
            ).astype(jnp.bfloat16)

        return branch_fn

    dec_grad = lax.switch(
        lax.axis_index("grp"), [make_branch(group) for group in range(group_count)]
    )
    partials = []
    for source in range(layers):
        total = jnp.zeros((derr.shape[0], dec_weight.shape[1]), jnp.float32)
        for index, (first, target) in enumerate(pairs):
            if first == source:
                total = total + jnp.einsum(
                    "rd,fd->rf",
                    derr[:, target, :],
                    dec_weight[index],
                    preferred_element_type=jnp.float32,
                )
        partials.append(total)
    dacts = lax.psum_scatter(
        jnp.stack(partials).astype(jnp.bfloat16), "layer", scatter_dimension=0, tiled=True
    ).astype(jnp.float32)[0]
    dpre = jnp.where(pre > 0, dacts, jnp.zeros_like(dacts))
    enc_bias_grad = lax.psum(jnp.sum(dpre, axis=0), "grp")[None]
    dpre_half = dpre.astype(jnp.bfloat16)
    block = rows
    enc_grad = lax.psum_scatter(
        jnp.einsum("rd,rf->df", block, dpre_half, preferred_element_type=jnp.float32).astype(
            jnp.bfloat16
        ),
        "grp",
        scatter_dimension=0,
        tiled=True,
    )[None]
    return (enc_grad, enc_bias_grad, dec_grad, dec_bias_grad)


def solution(mesh):
    return jax.shard_map(
        per_device,
        mesh=mesh,
        in_specs=(
            P("layer", ("grp", "feat"), None),
            P(("grp", "feat"), None, "layer"),
            P("layer", None, "feat"),
            P("layer", "feat"),
            P(None, "feat", "layer"),
            P(None, "layer"),
        ),
        out_specs=(
            P("layer", "grp", "feat"),
            P("layer", "feat"),
            P("grp", "feat", "layer"),
            P(None, "layer"),
        ),
        check_vma=False,
    )
```

profile of v0, /device:TPU:0, one launch (start us, length us, event | category | flops | bytes accessed | tf_op | source)
XLA Modules:
  0.0 584.9 jit_solution(11692224251480267616)
XLA Ops:
  7.2 0.7 all-gather.14.cloned.1.call-update
  7.9 21.8 %all-gather.14.cloned.1.call-done = bf16[1,256,2304]{2,1,0:T(8,128)(2,1)} async-done(((bf16[1,64,2304]{2,1,0:T(8,128)(2,1)}), bf16[1,256,2304]{2,1,0:T(8,128)(2,1)}) %all-gather.14.cloned.1.call-update) | async-done | bytes 1179664 | tf_op jit(solution)/shard_map/all_gather | solution.py:18
  29.7 7.5 %maximum_convert_fusion = (bf16[256,2048]{1,0:T(8,128)(2,1)}, f32[256,2048]{1,0:T(8,128)S(1)}) fusion(f32[2048]{0:T(1024)} %bitcast.235, bf16[1,2304,2048]{2,1,0:T(8,128)(2,1)} %param.10, bf16[1,256,2304]{2,1,0:T(8,128)(2,1)} %all-gather.14.cloned.1.call-done), kind=kOutput, calls=%fused_computation.126 | convolution fusion | flops 2417491968 | bytes 13770752 | tf_op jit(solution)/shard_map/dot_general | solution.py:19
  37.4 80.8 %all-gather.16.cloned.1.call-done = bf16[1024,2048]{1,0:T(8,128)(2,1)} async-done(((bf16[256,2048]{1,0:T(8,128)(2,1)}), bf16[1024,2048]{1,0:T(8,128)(2,1)}) %all-gather.16.cloned.1.call-update) | async-done | bytes 4194320 | tf_op jit(solution)/shard_map/all_gather | solution.py:21
  118.2 2.9 fusion.160
  121.1 3.4 fusion.97
  124.5 3.5 fusion.90
  128.0 2.8 fusion.80
  130.9 2.9 fusion.163
  134.1 0.8 fusion.131
  134.9 0.8 fusion.166
  135.7 0.8 fusion.137
  136.5 0.8 fusion.140
  137.3 0.8 fusion.169
  138.3 2.1 copy.28
  141.8 36.5 %all-reduce.3.cloned.1.call-done = bf16[256,4,576]{2,1,0:T(4,128)(2,1)} async-done(((bf16[256,4,576]{2,1,0:T(4,128)(2,1)}), bf16[256,4,576]{2,1,0:T(4,128)(2,1)}) %all-reduce.3.cloned.1.call-update) | async-done | bytes 1179664
  178.3 2.1 fusion.185
  180.7 18.1 %all-gather.8.cloned.1.call-done = bf16[256,4,576]{2,1,0:T(4,128)(2,1)} async-done(((bf16[64,4,576]{2,1,0:T(4,128)(2,1)}), bf16[256,4,576]{2,1,0:T(4,128)(2,1)}) %all-gather.8.cloned.1.call-update) | async-done | bytes 1179664 | tf_op jit(solution)/shard_map/all_gather | solution.py:40
  198.8 2.7 copy.29
  201.5 3.1 fusion.72
  204.6 2.7 fusion.85
  207.2 2.7 fusion.95
  209.9 2.7 fusion.102
  212.6 2.7 fusion.69
  215.2 2.7 convolution_add_fusion.2
  217.9 2.7 fusion.70
  220.6 2.7 convolution_add_fusion.5
  223.3 2.7 convolution_add_fusion.4
  225.9 2.7 fusion.71
  228.6 2.3 pad_maximum_fusion
  231.6 0.7 all-gather.10.cloned.1.call-update
  232.3 75.6 %reduce-scatter.5.cloned.1.call-done = bf16[1,256,2048]{2,1,0:T(8,128)(2,1)} async-done(((bf16[4,256,2048]{2,1,0:T(8,128)(2,1)}), bf16[1,256,2048]{2,1,0:T(8,128)(2,1)}) %reduce-scatter.5.cloned.1.call-update) | async-done | bytes 1048592 | tf_op jit(solution)/shard_map/reduce_scatter | solution.py:78
  307.9 1.8 fusion.106
  309.7 5.2 fusion.60
  314.9 12.9 %copy.35 = bf16[2304,2048]{1,0:T(8,128)(2,1)} copy(bf16[2304,2048]{0,1:T(8,128)(2,1)} %fusion.60) | data formatting | bytes 18874368
  327.9 24.8 %psum.15 = f32[4,576]{1,0:T(4,128)S(1)} all-reduce(f32[4,576]{1,0:T(4,128)S(1)} %get-tuple-element.59), channel_id=1, replica_groups=mesh['grp'=2,'layer'=4,'feat'=4] {'grp','feat'}, use_global_device_ids=true, to_apply=%region_8.9 | all-reduce | flops 2304 | bytes 18432 | tf_op jit(solution)/shard_map/psum | solution.py:39
  353.3 98.3 %all-gather.10.cloned.1.call-done = bf16[4,512,2048]{2,1,0:T(8,128)(2,1)} async-done(((bf16[4,256,2048]{2,1,0:T(8,128)(2,1)}), bf16[4,512,2048]{2,1,0:T(8,128)(2,1)}) %all-gather.10.cloned.1.call-update) | async-done | bytes 8388624 | tf_op jit(solution)/shard_map/all_gather | solution.py:41
  451.6 16.9 %conditional.6 = (bf16[5,2048,576]{1,2,0:T(8,128)(2,1)}) conditional(s32[]{:T(128)} %clamp.3, (bf16[4,512,2048]{2,1,0:T(8,128)(2,1)}, bf16[512,4,576]{0,2,1:T(8,128)(2,1)}) %tuple.24, (bf16[4,512,2048]{2,1,0:T(8,128)(2,1)}, bf16[512,4,576]{0,2,1:T(8,128)(2,1)}) %tuple.24), branch_computations={%region_5.0_spmd, %region_6.7_spmd} | conditional | flops 6045696000 | bytes 68223040
  451.6 4.7 fusion.1
  456.3 1.0 copy-done.8
  457.3 2.8 fusion.3
  460.1 2.8 fusion.5
  462.9 2.8 fusion.7
  465.7 2.8 fusion.9
  468.5 5.8 psum.14
  474.3 90.4 %reduce-scatter.7.cloned.1.call-done = bf16[1152,2048]{1,0:T(8,128)(2,1)} async-done(((bf16[2304,2048]{1,0:T(8,128)(2,1)}), bf16[1152,2048]{1,0:T(8,128)(2,1)}) %reduce-scatter.7.cloned.1.call-update) | async-done | bytes 4718608
  564.7 6.7 %copy.36 = bf16[1152,2048]{0,1:T(8,128)(2,1)} copy(bf16[1152,2048]{1,0:T(8,128)(2,1)} %reduce-scatter.7.cloned.1.call-done) | data formatting | bytes 9437184
  571.4 6.6 %copy.34 = bf16[1,1152,2048]{2,1,0:T(8,128)(2,1)} copy(bf16[1,1152,2048]{1,2,0:T(8,128)(2,1)} %bitcast.232) | data formatting | bytes 9437184
  (35 shorter events, 2.7 us)
Async XLA Ops:
  7.2 22.6 %all-gather.14.cloned.1.call-start = ((), (), s32[]{:S(2)}) async-start(), calls=%async_computation.6 | async-start | bytes 1474560 | tf_op jit(solution)/shard_map/all_gather | solution.py:18
  7.9 110.3 %all-gather.16.cloned.1.call-start = ((), (), s32[]{:S(2)}) async-start(), calls=%async_computation.7 | async-start | bytes 5242880 | tf_op jit(solution)/shard_map/all_gather | solution.py:21
  37.3 141.0 %all-reduce.3.cloned.1.call-start = ((), (), s32[]{:S(2)}) async-start(), calls=%async_computation.9 | async-start | bytes 2621440
  118.2 15.6 %copy-start.1 = (bf16[10,2048,576]{1,2,0:T(8,128)(2,1)S(1)}, bf16[10,2048,576]{1,2,0:T(8,128)(2,1)}, u32[]{:S(2)}) copy-start(bf16[10,2048,576]{1,2,0:T(8,128)(2,1)} %param.12) | copy-start | bytes 70778880
  130.8 3.2 copy-start.3
  138.3 2.2 copy-start.10
  138.3 40.0 %copy-start.5 = (f32[4,576]{1,0:T(4,128)S(1)}, f32[4,576]{1,0:T(4,128)}, u32[]{:S(2)}) copy-start(f32[4,576]{1,0:T(4,128)} %param.13) | copy-start | bytes 27652
  140.5 58.3 %all-gather.8.cloned.1.call-start = ((), (), s32[]{:S(2)}) async-start(), calls=%async_computation.2 | async-start | bytes 1638400 | tf_op jit(solution)/shard_map/all_gather | solution.py:40
  180.5 127.4 %reduce-scatter.5.cloned.1.call-start = ((), (), s32[]{:S(2)}) async-start(), calls=%async_computation.3 | async-start | bytes 5242880 | tf_op jit(solution)/shard_map/reduce_scatter | solution.py:78
  201.5 24.5 %copy-start = (bf16[256,4,576]{0,2,1:T(8,128)(2,1)}, bf16[256,4,576]{0,2,1:T(8,128)(2,1)S(1)}, u32[]{:S(2)}) copy-start(bf16[256,4,576]{0,2,1:T(8,128)(2,1)S(1)} %copy.29) | copy-start | bytes 3538948
  230.9 122.4 %all-gather.12.cloned.1.call-start = ((), (), s32[]{:S(2)}) async-start(), calls=%async_computation.5 | async-start | bytes 3538944 | tf_op jit(solution)/shard_map/all_gather | solution.py:42
  231.5 220.1 %all-gather.10.cloned.1.call-start = ((), (), s32[]{:S(2)}) async-start(), calls=%async_computation.4 | async-start | bytes 12582912 | tf_op jit(solution)/shard_map/all_gather | solution.py:41
  232.3 77.4 %copy-start.4 = (bf16[1,256,2304]{2,1,0:T(8,128)(2,1)S(1)}, bf16[1,256,2304]{2,1,0:T(8,128)(2,1)}, u32[]{:S(2)}) copy-start(bf16[1,256,2304]{2,1,0:T(8,128)(2,1)} %all-gather.14.cloned.1.call-done) | copy-start | bytes 3538948
  232.3 332.4 %reduce-scatter.7.cloned.1.call-start = ((), (), s32[]{:S(2)}) async-start(), calls=%async_computation.8 | async-start | bytes 14155776
  307.9 1.8 copy-start.2
  451.6 4.7 copy-start.6
  451.6 5.7 copy-start.8
Sparse Core Ops, SparseCore 0:
  9.5 20.1 all-gather.13
  37.4 80.7 all-gather.15
  140.6 37.6 all-reduce.2
  180.6 18.1 all-gather.7
  231.1 76.7 reduce-scatter.4
  309.3 36.7 all-gather.11
  347.6 103.9 all-gather.9
  453.9 110.7 reduce-scatter.6
where the time goes:
time: 586 us; the launch traced here: 585 us
  waiting for transfers between devices  423 us (72%)
  matrix products  75.4 us (13%)
  local copies, waits for them, and re-layouts  32.9 us (6%)
  blocking collectives  30.7 us (5%)
  between operations  15 us (3%)
  other arithmetic  7 us (1%)
    unnamed x10, waiting for transfers between devices  129 us
    all_gather x1, waiting for transfers between devices, per_device(): all_sources = lax.all_gather(sources, 'grp', axis=1, tiled=True)  98.3 us
    all_gather x1, waiting for transfers between devices, per_device(): sources = lax.all_gather(acts[None], 'layer', axis=0, tiled=True)  80.8 us
    reduce_scatter x1, waiting for transfers between devices, per_device(): lax.psum_scatter(jnp.stack(partials).astype(jnp.bfloat16), 'layer', scatt...  75.6 us
    unnamed x18, local copies, waits for them, and re-layouts  27.1 us
    dot_general x10, matrix products, per_device(): jnp.einsum('rd,fd->rf', derr[:, target, :], dec_weight[index], preferred_...  27.1 us
    psum x1, blocking collectives, per_device(): lax.psum(jnp.sum(errors, axis=0), ('grp', 'feat')) / total_tokens  24.8 us
    all_gather x1, waiting for transfers between devices, per_device(): rows = lax.all_gather(inputs[0], 'feat', axis=0, tiled=True)  21.8 us
  transfers between devices with their start and end apart: 8, of which 7 were waited for; matrix products, arithmetic and copies ran while one was open for 6% of the time, Pallas kernels for 0%

commit v1 on v0

v1 whole, which is shorter than its diff:
```python
import jax
import jax.numpy as jnp
from jax import lax
from jax.sharding import PartitionSpec as P


def pair_list(count):
    return [(source, target) for source in range(count) for target in range(source, count)]


def per_device(inputs, targets, enc_weight, enc_bias, dec_weight, dec_bias):
    layers = lax.axis_size("layer")
    feat_count = lax.axis_size("feat")
    group_count = lax.axis_size("grp")
    pairs = pair_list(layers)
    tok_dev, width = inputs.shape[1], inputs.shape[2]
    group_tokens = tok_dev * feat_count
    total_tokens = group_tokens * group_count
    block = dec_weight.shape[2]
    feats = dec_weight.shape[1]
    rows = lax.all_gather(inputs[0], "feat", axis=0, tiled=True)
    pre = jnp.dot(rows, enc_weight[0], preferred_element_type=jnp.float32) + enc_bias[0]
    acts = jnp.maximum(pre, 0.0).astype(jnp.bfloat16)
    sources = lax.all_gather(acts, "layer", axis=0, tiled=False)

    group = lax.axis_index("grp")
    own_width = width // group_count
    shifts = range(1, group_count)

    def shifted(value, shift):
        return lax.ppermute(
            value, "grp", [(g, (g + shift) % group_count) for g in range(group_count)]
        )

    def with_others(value, axis):
        return jnp.concatenate([value] + [shifted(value, k) for k in shifts], axis=axis)

    def column_block(shift):
        owner = lax.rem(group + shift, group_count)
        return lax.dynamic_slice_in_dim(rows, owner * own_width, own_width, axis=1)

    all_columns = jnp.concatenate(
        [column_block(0)] + [shifted(column_block(k), k) for k in shifts], axis=0
    )
    all_sources = with_others(sources, 1)

    def decode_target(target):
        total = jnp.zeros((group_tokens, block), jnp.float32)
        for index, (source, later) in enumerate(pairs):
            if later == target:
                total = total + jnp.dot(
                    sources[source], dec_weight[index], preferred_element_type=jnp.float32
                )
        return total.astype(jnp.bfloat16).reshape(feat_count, tok_dev, block)

    partial = jnp.stack([decode_target(target) for target in range(layers)], axis=1)
    recon = lax.psum_scatter(
        partial.reshape(feat_count * layers * tok_dev, block),
        "feat",
        scatter_dimension=0,
        tiled=True,
    )
    recon = recon.reshape(layers, tok_dev, block).astype(jnp.float32)
    wanted = jnp.swapaxes(targets, 0, 1).astype(jnp.float32)
    errors = recon + dec_bias[:, None, :] - wanted
    dec_bias_grad = lax.psum(jnp.sum(errors, axis=1), ("grp", "feat")) / total_tokens
    derr_own = (errors / total_tokens).astype(jnp.bfloat16)
    gathered = lax.all_gather(
        derr_own.reshape(layers * tok_dev, block), "feat", axis=0, tiled=True
    )
    gathered = gathered.reshape(feat_count, layers, tok_dev, block)
    derr = jnp.stack(
        [gathered[:, target].reshape(group_tokens, block) for target in range(layers)]
    )
    all_errors = with_others(derr, 1)
    per_group = len(pairs) // group_count

    partials = []
    for source in range(layers):
        total = jnp.zeros((group_tokens, feats), jnp.float32)
        for index, (first, target) in enumerate(pairs):
            if first == source:
                total = total + jnp.einsum(
                    "rd,fd->rf",
                    derr[target],
                    dec_weight[index],
                    preferred_element_type=jnp.float32,
                )
        partials.append(total.astype(jnp.bfloat16))
    dacts = lax.psum_scatter(
        jnp.concatenate(partials, axis=0), "layer", scatter_dimension=0, tiled=True
    ).astype(jnp.float32)
    dpre = jnp.where(pre > 0, dacts, jnp.zeros_like(dacts))
    enc_bias_grad = lax.psum(jnp.sum(dpre, axis=0), "grp")[None]
    all_dpre = with_others(dpre.astype(jnp.bfloat16), 0)

    starts = [group * per_group for group in range(group_count)]
    chosen_s = jnp.array([[s for s, _ in pairs[a : a + per_group]] for a in starts])
    chosen_t = jnp.array([[t for _, t in pairs[a : a + per_group]] for a in starts])

    def pair_grad(slot):
        left = lax.dynamic_index_in_dim(all_sources, chosen_s[group, slot], 0, False)
        right = lax.dynamic_index_in_dim(all_errors, chosen_t[group, slot], 0, False)
        return jnp.einsum("rf,rd->fd", left, right, preferred_element_type=jnp.float32).astype(
            jnp.bfloat16
        )

    dec_grad = jnp.stack([pair_grad(slot) for slot in range(per_group)])
    enc_grad = jnp.einsum(
        "rd,rf->df", all_columns, all_dpre, preferred_element_type=jnp.float32
    ).astype(jnp.bfloat16)[None]
    return (enc_grad, enc_bias_grad, dec_grad, dec_bias_grad)


def solution(mesh):
    return jax.shard_map(
        per_device,
        mesh=mesh,
        in_specs=(
            P("layer", ("grp", "feat"), None),
            P(("grp", "feat"), None, "layer"),
            P("layer", None, "feat"),
            P("layer", "feat"),
            P(None, "feat", "layer"),
            P(None, "layer"),
        ),
        out_specs=(
            P("layer", "grp", "feat"),
            P("layer", "feat"),
            P("grp", "feat", "layer"),
            P(None, "layer"),
        ),
        check_vma=False,
    )
```

time: 586 us -> 422 us (0.72)
  waiting for transfers between devices: 423 us -> 147 us
  blocking collectives: 30.7 us -> 128 us
  local copies, waits for them, and re-layouts: 32.9 us -> 11.6 us
  between operations: 15 us -> 32.6 us
  matrix products: 75.4 us -> 87.9 us
    unnamed x10 -> x5, waiting for transfers between devices: 129 us -> 0.75 us
    all_gather x4 -> x2, waiting for transfers between devices: 197 us -> 98.9 us  [the longest x1 80.8 us: per_device(): sources = lax.all_gather(acts, 'layer', axis=0, tiled=False)]
    psum x1, blocking collectives: 24.8 us -> 123 us  [per_device(): lax.psum(jnp.sum(errors, axis=1), ('grp', 'feat')) / total_tokens]
    reduce_scatter x1 -> x2, waiting for transfers between devices: 75.6 us -> 25 us  [the longest x1 25 us: per_device(): lax.psum_scatter(partial.reshape(feat_count * layers * tok_dev, block), '...]
    unnamed x18 -> x26, local copies, waits for them, and re-layouts: 27.1 us -> 2.11 us
    dot_general x26, matrix products: 67.8 us -> 79.6 us  [the longest x10 26.7 us: decode_target(): jnp.dot(sources[source], dec_weight[index], preferred_element_type=jnp.fl...]
  transfers between devices with their start and end apart: 8 -> 9, of which waited for: 7 -> 4; matrix products, arithmetic and copies ran while one was open for 6% -> 8% of each run, Pallas kernels for 0% -> 0%
where the time goes in v1:
time: 422 us; the launch traced here: 421 us
  waiting for transfers between devices  147 us (35%)
  blocking collectives  128 us (30%)
  matrix products  87.9 us (21%)
  between operations  32.6 us (8%)
  local copies, waits for them, and re-layouts  11.6 us (3%)
  other arithmetic  9.26 us (2%)
  starting transfers between devices  4.57 us (1%)
    psum x1, blocking collectives, per_device(): lax.psum(jnp.sum(errors, axis=1), ('grp', 'feat')) / total_tokens  123 us
    all_gather x1, waiting for transfers between devices, per_device(): sources = lax.all_gather(acts, 'layer', axis=0, tiled=False)  80.8 us
    dot_general x10, matrix products, decode_target(): jnp.dot(sources[source], dec_weight[index], preferred_element_type=jnp.fl...  26.7 us
    dot_general x10, matrix products, per_device(): jnp.einsum('rd,fd->rf', derr[target], dec_weight[index], preferred_elemen...  26.6 us
    reduce_scatter x1, waiting for transfers between devices, per_device(): lax.psum_scatter(partial.reshape(feat_count * layers * tok_dev, block), '...  25 us
    all_gather x1, waiting for transfers between devices, per_device(): rows = lax.all_gather(inputs[0], 'feat', axis=0, tiled=True)  21.8 us
    dot_general x5, matrix products, pair_grad(): jnp.einsum('rf,rd->fd', left, right, preferred_element_type=jnp.float32)  21 us
    all_gather x1, waiting for transfers between devices, per_device(): lax.all_gather(derr_own.reshape(layers * tok_dev, block), 'feat', axis=0,...  18.1 us
  transfers between devices with their start and end apart: 9, of which 4 were waited for; matrix products, arithmetic and copies ran while one was open for 8% of the time, Pallas kernels for 0%

profile of v1, /device:TPU:0, one launch (start us, length us, event | category | flops | bytes accessed | tf_op | source)
XLA Modules:
  0.0 421.0 jit_solution(9382348462270128046)
XLA Ops:
  7.2 0.7 all-gather.8.cloned.1.call-update
  7.9 21.8 %all-gather.8.cloned.1.call-done = bf16[1,256,2304]{2,1,0:T(8,128)(2,1)} async-done(((bf16[1,64,2304]{2,1,0:T(8,128)(2,1)}), bf16[1,256,2304]{2,1,0:T(8,128)(2,1)}) %all-gather.8.cloned.1.call-update) | async-done | bytes 1179664 | tf_op jit(solution)/shard_map/all_gather | solution.py:21
  29.7 8.3 %maximum_convert_fusion = (bf16[256,2048]{1,0:T(8,128)(2,1)}, f32[256,2048]{1,0:T(8,128)}) fusion(f32[2048]{0:T(1024)} %bitcast.230, bf16[1,2304,2048]{2,1,0:T(8,128)(2,1)} %param.10, bf16[1,256,2304]{2,1,0:T(8,128)(2,1)} %all-gather.8.cloned.1.call-done), kind=kOutput, calls=%fused_computation.91 | convolution fusion | flops 2417491968 | bytes 13770752 | tf_op jit(solution)/shard_map/dot_general | solution.py:22
  38.1 80.8 %all-gather.10.cloned.1.call-done = bf16[1024,2048]{1,0:T(8,128)(2,1)} async-done(((bf16[256,2048]{1,0:T(8,128)(2,1)}), bf16[1024,2048]{1,0:T(8,128)(2,1)}) %all-gather.10.cloned.1.call-update) | async-done | bytes 4194320 | tf_op jit(solution)/shard_map/all_gather | solution.py:24
  118.9 2.9 fusion.26
  122.1 2.5 fusion.101
  124.6 2.5 fusion.104
  127.1 2.5 fusion.110
  129.8 2.9 fusion.36
  133.0 2.5 fusion.95
  135.5 2.5 fusion.113
  138.2 2.8 fusion.43
  141.0 2.8 fusion.116
  144.0 2.8 fusion.119
  147.3 1.2 copy.32
  148.6 25.0 %reduce-scatter.3.cloned.1.call-done = bf16[256,576]{1,0:T(8,128)(2,1)} async-done(((bf16[1024,576]{1,0:T(8,128)(2,1)}), bf16[256,576]{1,0:T(8,128)(2,1)}) %reduce-scatter.3.cloned.1.call-update) | async-done | bytes 294928 | tf_op jit(solution)/shard_map/reduce_scatter | solution.py:57
  173.6 1.8 fusion.147
  175.7 18.1 %all-gather.6.cloned.1.call-done = bf16[1024,576]{1,0:T(8,128)(2,1)} async-done(((bf16[256,576]{1,0:T(8,128)(2,1)}), bf16[1024,576]{1,0:T(8,128)(2,1)}) %all-gather.6.cloned.1.call-update) | async-done | bytes 1179664 | tf_op jit(solution)/shard_map/all_gather | solution.py:68
  193.8 1.4 fusion.159
  195.2 2.6 fusion.48
  197.9 2.6 fusion.41
  200.5 2.7 convolution_add_fusion.5
  203.2 2.6 fusion.31
  205.9 2.7 convolution_add_fusion.4
  208.5 2.6 convolution_convert_fusion.6
  211.2 2.6 fusion.16
  213.9 2.7 convolution_add_fusion.2
  216.5 2.7 fusion.17
  219.2 2.7 fusion.18
  221.9 2.3 pad_maximum_fusion
  224.2 1.5 collective-permute-start.2
  226.0 1.4 copy.38
  228.0 0.7 constant_dynamic-slice_fusion.4
  247.2 2.4 dynamic-slice_bitcast_fusion.1
  249.6 1.5 collective-permute-start
  251.0 122.9 %psum.15 = f32[4,576]{1,0:T(4,128)S(1)} all-reduce(f32[4,576]{1,0:T(4,128)S(1)} %get-tuple-element.12), channel_id=1, replica_groups=mesh['grp'=2,'layer'=4,'feat'=4] {'grp','feat'}, use_global_device_ids=true, to_apply=%region_5.6 | all-reduce | flops 2304 | bytes 18432 | tf_op jit(solution)/shard_map/psum | solution.py:66
  374.5 1.7 copy.39
  376.2 1.8 pad_maximum_fusion.1
  378.1 1.5 copy-done.1
  379.6 4.1 fusion.4
  383.7 1.9 fusion.70
  385.9 0.6 collective-permute-start.1
  386.5 4.7 %fusion.6 = bf16[5,2048,576]{1,2,0:T(8,128)(2,1)} fusion(bf16[5,2048,576]{1,2,0:T(8,128)(2,1)} %fusion.4, s32[]{:T(128)S(6)} %select_n.60, bf16[4,256,2048]{2,1,0:T(8,128)(2,1)} %bitcast.225, bf16[4,256,2048]{2,1,0:T(8,128)(2,1)} %collective-permute-done.2, bf16[4,512,576]{2,1,0:T(8,128)(2,1)S(1)} %copy-done.2, s32[]{:T(128)S(6)} %select_n.61), kind=kOutput, calls=%fused_computation.23 | convolution fusion | flops 1213333504 | bytes 11403272 | tf_op jit(solution)/shard_map/rf,rd->fd/dot_general | solution.py:104
  391.2 4.1 fusion.8
  395.3 4.1 fusion.10
  399.4 4.1 fusion.12
  403.5 5.6 %psum.14 = f32[1,2048]{1,0:T(1,128)} all-reduce(f32[1,2048]{1,0:T(1,128)S(1)} %bitcast.223), channel_id=1, replica_groups=mesh['grp'=2,'layer'=4,'feat'=4] {'grp'}, use_global_device_ids=true, to_apply=%region_3.0 | all-reduce | flops 2048 | bytes 16384 | tf_op jit(solution)/shard_map/psum | solution.py:94
  409.1 5.3 %fusion.2 = bf16[1,1152,2048]{2,1,0:T(8,128)(2,1)} fusion(bf16[256,2048]{1,0:T(8,128)(2,1)S(1)} %collective-permute-done.1, bf16[256,2048]{1,0:T(8,128)(2,1)S(1)} %fusion.71, bf16[256,1152]{1,0:T(8,128)(2,1)} %collective-permute-done, bf16[256,1152]{1,0:T(8,128)(2,1)S(1)} %copy-done.4), kind=kOutput, calls=%fused_computation.13 | convolution fusion | flops 2424832000 | bytes 7995392 | tf_op jit(solution)/shard_map/rd,rf->df/dot_general | solution.py:109
  (48 shorter events, 3.9 us)
Async XLA Ops:
  7.2 22.6 %all-gather.8.cloned.1.call-start = ((), (), s32[]{:S(2)}) async-start(), calls=%async_computation.5 | async-start | bytes 1474560 | tf_op jit(solution)/shard_map/all_gather | solution.py:21
  7.9 111.0 %all-gather.10.cloned.1.call-start = ((), (), s32[]{:S(2)}) async-start(), calls=%async_computation.6 | async-start | bytes 5242880 | tf_op jit(solution)/shard_map/all_gather | solution.py:24
  38.0 135.6 %reduce-scatter.3.cloned.1.call-start = ((), (), s32[]{:S(2)}) async-start(), calls=%async_computation.2 | async-start | bytes 1638400 | tf_op jit(solution)/shard_map/reduce_scatter | solution.py:57
  118.9 3.2 copy-start.9
  129.8 3.2 copy-start.10
  147.3 26.3 %copy-start.5 = (bf16[64,4,576]{2,1,0:T(4,128)(2,1)S(1)}, bf16[64,4,576]{2,1,0:T(4,128)(2,1)}, u32[]{:S(2)}) copy-start(bf16[64,4,576]{2,1,0:T(4,128)(2,1)} %param.9) | copy-start | bytes 884740
  147.3 26.3 %copy-start.6 = (f32[4,576]{1,0:T(4,128)S(1)}, f32[4,576]{1,0:T(4,128)}, u32[]{:S(2)}) copy-start(f32[4,576]{1,0:T(4,128)} %param.13) | copy-start | bytes 27652
  148.5 45.3 %all-gather.6.cloned.1.call-start = ((), (), s32[]{:S(2)}) async-start(), calls=%async_computation.3 | async-start | bytes 1638400 | tf_op jit(solution)/shard_map/all_gather | solution.py:68
  175.5 208.2 %reduce-scatter.5.cloned.1.call-start = ((), (), s32[]{:S(2)}) async-start(), calls=%async_computation.4 | async-start | bytes 5242880 | tf_op jit(solution)/shard_map/reduce_scatter | solution.py:90
  224.2 3.8 copy-start.7
  224.2 3.8 copy-start.8
  224.2 153.8 %collective-permute-start.2 = (bf16[4,256,2048]{2,1,0:T(8,128)(2,1)}, bf16[4,256,2048]{2,1,0:T(8,128)(2,1)}, u32[]{:S(2)}, u32[]{:S(2)}) collective-permute-start(bf16[4,256,2048]{2,1,0:T(8,128)(2,1)} %bitcast.224), channel_id=1, source_target_pairs={{0,16},{16,0},{1,17},{17,1},{2,18},{18,2},{3,19},{19,3},{4,20},{20... | collective-permute-start | bytes 12582920 | tf_op jit(solution)/shard_map/ppermute | solution.py:31
  227.5 147.1 %collective-permute-start.3 = (bf16[4,256,576]{1,2,0:T(8,128)(2,1)}, bf16[4,256,576]{1,2,0:T(8,128)(2,1)}, u32[]{:S(2)}, u32[]{:S(2)}) collective-permute-start(bf16[4,256,576]{1,2,0:T(8,128)(2,1)} %copy.38), channel_id=1, source_target_pairs={{0,16},{16,0},{1,17},{17,1},{2,18},{18,2},{3,19},{19,3},{4,20},{20... | collective-permute-start | bytes 3538952 | tf_op jit(solution)/shard_map/ppermute | solution.py:31
  249.6 159.5 %collective-permute-start = (bf16[256,1152]{1,0:T(8,128)(2,1)}, bf16[256,1152]{1,0:T(8,128)(2,1)}, u32[]{:S(2)}, u32[]{:S(2)}) collective-permute-start(bf16[256,1152]{1,0:T(8,128)(2,1)} %get-tuple-element.11), channel_id=1, source_target_pairs={{0,16},{16,0},{1,17},{17,1},{2,18},{18,2},{3,19},{19,3},{4,20},{20... | collective-permute-start | bytes 1769480 | tf_op jit(solution)/shard_map/ppermute | solution.py:31
  376.2 3.4 copy-start.11
  378.0 1.6 copy-start.1
  378.0 5.6 %copy-start.3 = (f32[256,2048]{1,0:T(8,128)S(1)}, f32[256,2048]{1,0:T(8,128)}, u32[]{:S(2)}) copy-start(f32[256,2048]{1,0:T(8,128)} %get-tuple-element.25) | copy-start | bytes 6291460
  383.7 1.9 copy-start
  383.7 2.9 copy-start.2
  385.9 5.3 %copy-start.12 = (bf16[1024,2048]{1,0:T(8,128)(2,1)S(1)}, bf16[1024,2048]{1,0:T(8,128)(2,1)}, u32[]{:S(2)}) copy-start(bf16[1024,2048]{1,0:T(8,128)(2,1)} %all-gather.10.cloned.1.call-done) | copy-start | bytes 12582916
  385.9 23.2 %collective-permute-start.1 = (bf16[256,2048]{1,0:T(8,128)(2,1)S(1)}, bf16[256,2048]{1,0:T(8,128)(2,1)S(1)}, u32[]{:S(2)}, u32[]{:S(2)}) collective-permute-start(bf16[256,2048]{1,0:T(8,128)(2,1)S(1)} %fusion.71), channel_id=1, source_target_pairs={{0,16},{16,0},{1,17},{17,1},{2,18},{18,2},{3,19},{19,3},{4,20},{20... | collective-permute-start | bytes 3145736 | tf_op jit(solution)/shard_map/ppermute | solution.py:31
  399.4 9.7 %copy-start.4 = (bf16[256,1152]{1,0:T(8,128)(2,1)S(1)}, bf16[256,1152]{1,0:T(8,128)(2,1)}, u32[]{:S(2)}) copy-start(bf16[256,1152]{1,0:T(8,128)(2,1)} %get-tuple-element.10) | copy-start | bytes 1769476
Sparse Core Ops, SparseCore 0:
  9.5 20.1 all-gather.7
  38.2 80.7 all-gather.9
  148.7 24.9 reduce-scatter.2
  175.6 18.1 all-gather.5
  224.3 76.8 reduce-scatter.4
